TPU v7x, 32 devices: a whole 2x2x4 slice. The times are simulated.
32 devices in a mesh: grp: 4 (over z), row: 4 (over y, core), col: 2 (over x).
Axes of the slice: x: 2, y: 2, z: 4, core: 2. Of those that a mesh axis runs over, the one named last changes fastest.
Arguments:
- tokens: bfloat16 [2048, 4608], P(('grp', 'row', 'col')), parts along dimension 0, may hold values from -6 to 6
- ln_gain: float32 [4608], replicated, may hold values from 0.1 to 1.9
- w_in: bfloat16 [4608, 12288], P('row', 'col'), may hold values from -0.09375 to 0.09375
- b_in: float32 [12288], P('col'), may hold values from -3 to 3
- w_out: bfloat16 [12288, 4608], P('col', 'row'), may hold values from -0.0546875 to 0.0546875
- b_out: float32 [4608], P('row'), may hold values from -3 to 3
Outputs:
- result: bfloat16 [2048, 4608], P(('grp', 'row', 'col')), parts along dimension 0
There are 4 independent parts, one for each index of `grp`. A program takes and returns all parts, laid end to end along the dimension named above; an argument that names none is the same for every part. Nothing has to cross between parts.
All inputs are finite; a program needn't handle non-finite values.
Results may differ from a plain program's by a relative error of at most 0.0095.
Values may be sent and summed in bfloat16 or wider, within the bound.
No kernel may reach another device: no remote copies, remote signals or barrier semaphores. Data moves between devices by JAX's collectives and lax.ppermute only.
A program may use at most 128 MiB of HBM per device.

v0:
```python
import jax
import jax.numpy as jnp
from jax import lax
from jax.sharding import PartitionSpec as P


def swap(value, axis, size, mask):
    return lax.ppermute(value, axis, [(i, i ^ mask) for i in range(size)])


def pick(blocks, index, slot):
    bits = len(blocks).bit_length() - 1

    def choose(bit, done):
        if bit == bits:
            return blocks[slot ^ done]
        on = (index >> bit) & 1
        return jnp.where(on == 1, choose(bit + 1, done | (1 << bit)), choose(bit + 1, done))

    return choose(0, 0)


def solution(mesh):
    rows, cols = mesh.shape["row"], mesh.shape["col"]
    low_bits = rows.bit_length() - 2
    top = rows // 2
    near = [0]
    for bit in reversed(range(low_bits)):
        near = near + [p | (1 << bit) for p in near]
    far = [p | top for p in near]

    def low_reduce(value):
        for bit in range(low_bits):
            half = value.shape[0] // 2
            got = swap(value[half:], "row", rows, 1 << bit)
            value = (value[:half].astype(jnp.float32) + got.astype(jnp.float32)).astype(jnp.bfloat16)
        return value

    def low_gather(value):
        for bit in reversed(range(low_bits)):
            value = jnp.concatenate([value, swap(value, "row", rows, 1 << bit)])
        return value

    def local(tokens, ln_gain, w_in, b_in, w_out, b_out):
        width = w_in.shape[0]
        row = lax.axis_index("row")
        values = tokens.astype(jnp.float32)
        row_mean = jnp.mean(values, axis=1, keepdims=True)
        centered = values - row_mean
        row_var = jnp.mean(centered * centered, axis=1, keepdims=True)
        normed = (centered * lax.rsqrt(row_var + 1e-06) * ln_gain).astype(jnp.bfloat16)

        def slab(p):
            return lax.dynamic_slice_in_dim(normed, (row ^ p) * width, width, axis=1)

        near_own = jnp.concatenate([slab(p) if p == 0 else swap(slab(p), "row", rows, p) for p in near])
        far_own = jnp.concatenate([swap(slab(p), "row", rows, p) for p in far])
        near_in = [near_own if q == 0 else swap(near_own, "col", cols, q) for q in range(cols)]
        far_in = [far_own if q == 0 else swap(far_own, "col", cols, q) for q in range(cols)]

        full = w_in.shape[1]
        whole = [slice(0, full)]
        halves = [slice(0, full // 2), slice(full // 2, full)]

        def up(panel, cut):
            return jnp.dot(panel, w_in[:, cut], preferred_element_type=jnp.float32).astype(jnp.bfloat16)

        def down(hidden, cut):
            return jnp.dot(hidden, w_out[cut], preferred_element_type=jnp.float32)

        near_out, far_out = [None] * cols, [None] * cols
        hidden = [None] * cols
        for q in range(cols):
            cuts = halves if q == 0 else whole
            hidden[q] = []
            for cut in cuts:
                away = swap(low_reduce(up(near_in[q], cut)), "row", rows, top)
                kept = low_reduce(up(far_in[q], cut))
                preact = kept.astype(jnp.float32) + away.astype(jnp.float32) + b_in[cut]
                hidden[q].append(jax.nn.gelu(preact, approximate=False).astype(jnp.bfloat16))
            far_out[q] = sum(down(low_gather(h), cut) for h, cut in zip(hidden[q], cuts))
        for q in reversed(range(cols)):
            cuts = halves if q == 0 else whole
            near_out[q] = sum(down(low_gather(swap(h, "row", rows, top)), cut) for h, cut in zip(hidden[q], cuts))

        def finish(parts):
            total = parts[0]
            for q in range(1, cols):
                total = total + swap(parts[q].astype(jnp.bfloat16), "col", cols, q).astype(jnp.float32)
            return (total + b_out).astype(jnp.bfloat16)

        blocks = {}
        own = tokens.shape[0]
        for names, branch in ((far, finish(far_out)), (near, finish(near_out))):
            for place, p in enumerate(names):
                block = branch[place * own : (place + 1) * own]
                blocks[p] = block if p == 0 else swap(block, "row", rows, p)
        regrouped = jnp.concatenate([pick(blocks, row, s) for s in range(rows)], axis=1)
        return (values + regrouped.astype(jnp.float32)).astype(jnp.bfloat16)

    in_specs = (
        P(("grp", "row", "col"), None),
        P(),
        P("row", "col"),
        P("col"),
        P("col", "row"),
        P("row"),
    )
    out_specs = P(("grp", "row", "col"), None)

    return jax.shard_map(local, mesh=mesh, in_specs=in_specs, out_specs=out_specs, check_vma=False)
```

profile of v0, /device:TPU:0, one launch (start us, length us, event | category | flops | bytes accessed | tf_op | source)
XLA Modules:
  0.0 126.7 jit_solution(944321078774414495)
XLA Ops:
  4.5 2.6 %collective-permute-start = (bf16[64,1152]{1,0:T(8,128)(2,1)S(1)}, bf16[64,1152]{1,0:T(8,128)(2,1)S(1)}, u32[]{:S(2)}, u32[]{:S(2)}) collective-permute-start(bf16[64,1152]{1,0:T(8,128)(2,1)S(1)} %get-tuple-element.12), channel_id=1, source_target_pairs={{0,4},{2,6},{4,0},{6,2},{1,5},{3,7},{5,1},{7,3},{8,12},{10,14},{12... | collective-permute-start | bytes 442376 | tf_op jit(solution)/shard_map/ppermute | solution.py:8
  7.2 1.8 %collective-permute-start.13 = (bf16[128,1152]{1,0:T(8,128)(2,1)S(1)}, bf16[128,1152]{1,0:T(8,128)(2,1)S(1)}, u32[]{:S(2)}, u32[]{:S(2)}) collective-permute-start(bf16[128,1152]{1,0:T(8,128)(2,1)S(1)} %pad_maximum_fusion), channel_id=1, source_target_pairs={{0,1},{1,0},{2,3},{3,2},{4,5},{5,4},{6,7},{7,6},{8,9},{9,8},{10,11... | collective-permute-start | bytes 884744 | tf_op jit(solution)/shard_map/ppermute | solution.py:8
  9.0 2.8 %collective-permute-done = bf16[64,1152]{1,0:T(8,128)(2,1)S(1)} collective-permute-done((bf16[64,1152]{1,0:T(8,128)(2,1)S(1)}, bf16[64,1152]{1,0:T(8,128)(2,1)S(1)}, u32[]{:S(2)}, u32[]{:S(2)}) %collective-permute-start) | collective-permute-done | bytes 147488 | tf_op jit(solution)/shard_map/ppermute | solution.py:8
  11.8 2.6 %collective-permute-done.1 = bf16[64,1152]{1,0:T(8,128)(2,1)S(1)} collective-permute-done((bf16[64,1152]{1,0:T(8,128)(2,1)S(1)}, bf16[64,1152]{1,0:T(8,128)(2,1)S(1)}, u32[]{:S(2)}, u32[]{:S(2)}) %collective-permute-start.1) | collective-permute-done | bytes 147488 | tf_op jit(solution)/shard_map/ppermute | solution.py:8
  16.0 4.2 %fusion.22 = bf16[128,3072]{1,0:T(8,128)(2,1)S(1)} fusion(bf16[128,1152]{1,0:T(8,128)(2,1)S(1)} %constant_dynamic-update-slice_fusion, bf16[1152,6144]{1,0:T(8,128)(2,1)} %param.8), kind=kOutput, calls=%fused_computation.20 | convolution fusion | flops 906362880 | bytes 8159232 | tf_op jit(solution)/shard_map/dot_general | solution.py:66
  25.2 2.2 %convolution_convert_fusion = bf16[128,6144]{1,0:T(8,128)(2,1)S(1)} fusion(bf16[128,1152]{1,0:T(8,128)(2,1)S(1)} %collective-permute-done.13, bf16[1152,6144]{1,0:T(8,128)(2,1)S(1)} %copy-done), kind=kOutput, calls=%fused_computation | convolution fusion | flops 1812725760 | bytes 16023552 | tf_op jit(solution)/shard_map/dot_general | solution.py:66
  28.0 2.2 %convolution_convert_fusion.1 = bf16[128,6144]{1,0:T(8,128)(2,1)S(1)} fusion(bf16[128,1152]{1,0:T(8,128)(2,1)S(1)} %collective-permute-done.11, bf16[1152,6144]{1,0:T(8,128)(2,1)S(1)} %copy-done), kind=kOutput, calls=%fused_computation.1 | convolution fusion | flops 1812725760 | bytes 16023552 | tf_op jit(solution)/shard_map/dot_general | solution.py:66
  30.6 1.6 %collective-permute-start.9 = (bf16[64,3072]{1,0:T(8,128)(2,1)S(1)}, bf16[64,3072]{1,0:T(8,128)(2,1)S(1)}, u32[]{:S(2)}, u32[]{:S(2)}) collective-permute-start(bf16[64,3072]{1,0:T(8,128)(2,1)S(1)} %add_convert_fusion.2), channel_id=1, source_target_pairs={{0,4},{2,6},{4,0},{6,2},{1,5},{3,7},{5,1},{7,3},{8,12},{10,14},{12... | collective-permute-start | bytes 1179656 | tf_op jit(solution)/shard_map/ppermute | solution.py:8
  33.0 1.6 %collective-permute-start.15 = (bf16[64,6144]{1,0:T(8,128)(2,1)S(1)}, bf16[64,6144]{1,0:T(8,128)(2,1)S(1)}, u32[]{:S(2)}, u32[]{:S(2)}) collective-permute-start(bf16[64,6144]{1,0:T(8,128)(2,1)S(1)} %add_convert_fusion), channel_id=1, source_target_pairs={{0,4},{2,6},{4,0},{6,2},{1,5},{3,7},{5,1},{7,3},{8,12},{10,14},{12... | collective-permute-start | bytes 2359304 | tf_op jit(solution)/shard_map/ppermute | solution.py:8
  34.6 8.0 %collective-permute-done.9 = bf16[64,3072]{1,0:T(8,128)(2,1)S(1)} collective-permute-done((bf16[64,3072]{1,0:T(8,128)(2,1)S(1)}, bf16[64,3072]{1,0:T(8,128)(2,1)S(1)}, u32[]{:S(2)}, u32[]{:S(2)}) %collective-permute-start.9) | collective-permute-done | bytes 393248 | tf_op jit(solution)/shard_map/ppermute | solution.py:8
  42.6 2.0 %fusion.79 = bf16[64,3072]{1,0:T(8,128)(2,1)S(1)} fusion(bf16[64,3072]{1,0:T(8,128)(2,1)S(1)} %collective-permute-done.9, bf16[64,3072]{1,0:T(8,128)(2,1)S(1)} %collective-permute-done.7, bf16[128,3072]{1,0:T(8,128)(2,1)S(1)} %fusion.22, f32[3072]{0:T(1024)S(1)} %get-tuple-element.16), kind=kLoop, calls=%fused_computation.76 | loop fusion | flops 14352384 | bytes 1585152 | tf_op jit(solution)/shard_map/convert_element_type | solution.py:80
  44.6 1.6 %collective-permute-start.21 = (bf16[64,3072]{1,0:T(8,128)(2,1)S(1)}, bf16[64,3072]{1,0:T(8,128)(2,1)S(1)}, u32[]{:S(2)}, u32[]{:S(2)}) collective-permute-start(bf16[64,3072]{1,0:T(8,128)(2,1)S(1)} %fusion.79), channel_id=1, source_target_pairs={{0,4},{2,6},{4,0},{6,2},{1,5},{3,7},{5,1},{7,3},{8,12},{10,14},{12... | collective-permute-start | bytes 1179656 | tf_op jit(solution)/shard_map/ppermute | solution.py:8
  46.2 4.8 %collective-permute-done.5 = bf16[64,3072]{1,0:T(8,128)(2,1)S(1)} collective-permute-done((bf16[64,3072]{1,0:T(8,128)(2,1)S(1)}, bf16[64,3072]{1,0:T(8,128)(2,1)S(1)}, u32[]{:S(2)}, u32[]{:S(2)}) %collective-permute-start.5) | collective-permute-done | bytes 393248 | tf_op jit(solution)/shard_map/ppermute | solution.py:8
  51.1 1.8 %fusion.76 = bf16[64,3072]{1,0:T(8,128)(2,1)S(1)} fusion(bf16[64,3072]{1,0:T(8,128)(2,1)S(1)} %collective-permute-done.5, bf16[64,3072]{1,0:T(8,128)(2,1)S(1)} %collective-permute-done.2, bf16[128,3072]{1,0:T(8,128)(2,1)S(1)} %fusion.16, f32[3072]{0:T(1024)S(1)} %get-tuple-element.15), kind=kLoop, calls=%fused_computation.73 | loop fusion | flops 14352384 | bytes 1585152 | tf_op jit(solution)/shard_map/convert_element_type | solution.py:80
  54.5 13.4 %collective-permute-done.15 = bf16[64,6144]{1,0:T(8,128)(2,1)S(1)} collective-permute-done((bf16[64,6144]{1,0:T(8,128)(2,1)S(1)}, bf16[64,6144]{1,0:T(8,128)(2,1)S(1)}, u32[]{:S(2)}, u32[]{:S(2)}) %collective-permute-start.15) | collective-permute-done | bytes 786464 | tf_op jit(solution)/shard_map/ppermute | solution.py:8
  67.9 3.7 %fusion.54 = bf16[64,6144]{1,0:T(8,128)(2,1)S(1)} fusion(bf16[64,6144]{1,0:T(8,128)(2,1)S(1)} %collective-permute-done.15, bf16[64,6144]{1,0:T(8,128)(2,1)S(1)} %collective-permute-done.12, bf16[128,6144]{1,0:T(8,128)(2,1)S(1)} %convolution_convert_fusion.1, f32[6144]{0:T(1024)S(1)} %copy-done.2), kind=kLoop, calls=%fused_computation.38 | loop fusion | flops 28704768 | bytes 3170304 | tf_op jit(solution)/shard_map/convert_element_type | solution.py:80
  72.2 4.2 %collective-permute-done.21 = bf16[64,3072]{1,0:T(8,128)(2,1)S(1)} collective-permute-done((bf16[64,3072]{1,0:T(8,128)(2,1)S(1)}, bf16[64,3072]{1,0:T(8,128)(2,1)S(1)}, u32[]{:S(2)}, u32[]{:S(2)}) %collective-permute-start.21) | collective-permute-done | bytes 393248 | tf_op jit(solution)/shard_map/ppermute | solution.py:8
  76.3 7.8 %collective-permute-done.19 = bf16[64,3072]{1,0:T(8,128)(2,1)S(1)} collective-permute-done((bf16[64,3072]{1,0:T(8,128)(2,1)S(1)}, bf16[64,3072]{1,0:T(8,128)(2,1)S(1)}, u32[]{:S(2)}, u32[]{:S(2)}) %collective-permute-start.19) | collective-permute-done | bytes 393248 | tf_op jit(solution)/shard_map/ppermute | solution.py:8
  84.2 4.4 %fusion.2 = f32[128,1152]{1,0:T(8,128)S(1)} fusion(bf16[6144,1152]{1,0:T(8,128)(2,1)} %param.10, bf16[64,3072]{1,0:T(8,128)(2,1)S(1)} %collective-permute-done.10, bf16[64,3072]{1,0:T(8,128)(2,1)S(1)} %fusion.79), kind=kOutput, calls=%fused_computation.4 | convolution fusion | flops 907542528 | bytes 8454144 | tf_op jit(solution)/shard_map/dot_general | solution.py:69
  90.2 7.3 %convolution_convert_fusion.3 = bf16[128,1152]{1,0:T(8,128)(2,1)S(1)} fusion(bf16[6144,1152]{1,0:T(8,128)(2,1)} %param.10, bf16[64,6144]{1,0:T(8,128)(2,1)S(1)} %collective-permute-done.16, bf16[64,6144]{1,0:T(8,128)(2,1)S(1)} %fusion.54), kind=kOutput, calls=%fused_computation.31 | convolution fusion | flops 1815232512 | bytes 16023552 | tf_op jit(solution)/shard_map/dot_general | solution.py:69
  98.0 10.6 %collective-permute-done.23 = bf16[64,6144]{1,0:T(8,128)(2,1)S(1)} collective-permute-done((bf16[64,6144]{1,0:T(8,128)(2,1)S(1)}, bf16[64,6144]{1,0:T(8,128)(2,1)S(1)}, u32[]{:S(2)}, u32[]{:S(2)}) %collective-permute-start.23) | collective-permute-done | bytes 786464 | tf_op jit(solution)/shard_map/ppermute | solution.py:8
  111.2 2.2 %convolution_convert_fusion.2 = bf16[128,1152]{1,0:T(8,128)(2,1)S(1)} fusion(bf16[6144,1152]{1,0:T(8,128)(2,1)S(1)} %bitcast.9, bf16[64,6144]{1,0:T(8,128)(2,1)S(1)} %collective-permute-done.24, bf16[64,6144]{1,0:T(8,128)(2,1)S(1)} %collective-permute-done.23), kind=kOutput, calls=%fused_computation.30 | convolution fusion | flops 1815232512 | bytes 16023552 | tf_op jit(solution)/shard_map/dot_general | solution.py:69
  113.9 1.6 %collective-permute-start.18 = (bf16[64,1152]{1,0:T(8,128)(2,1)S(1)}, bf16[64,1152]{1,0:T(8,128)(2,1)S(1)}, u32[]{:S(2)}, u32[]{:S(2)}) collective-permute-start(bf16[64,1152]{1,0:T(8,128)(2,1)S(1)} %get-tuple-element.14), channel_id=1, source_target_pairs={{0,6},{2,4},{4,2},{6,0},{1,7},{3,5},{5,3},{7,1},{8,14},{10,12},{12... | collective-permute-start | bytes 442376 | tf_op jit(solution)/shard_map/ppermute | solution.py:8
  115.8 7.2 %collective-permute-done.25 = bf16[128,1152]{1,0:T(8,128)(2,1)S(1)} collective-permute-done((bf16[128,1152]{1,0:T(8,128)(2,1)S(1)}, bf16[128,1152]{1,0:T(8,128)(2,1)S(1)}, u32[]{:S(2)}, u32[]{:S(2)}) %collective-permute-start.25) | collective-permute-done | bytes 294944 | tf_op jit(solution)/shard_map/ppermute | solution.py:8
  (87 shorter events, 23.9 us)
Async XLA Ops:
  4.5 7.3 %collective-permute-start = (bf16[64,1152]{1,0:T(8,128)(2,1)S(1)}, bf16[64,1152]{1,0:T(8,128)(2,1)S(1)}, u32[]{:S(2)}, u32[]{:S(2)}) collective-permute-start(bf16[64,1152]{1,0:T(8,128)(2,1)S(1)} %get-tuple-element.12), channel_id=1, source_target_pairs={{0,4},{2,6},{4,0},{6,2},{1,5},{3,7},{5,1},{7,3},{8,12},{10,14},{12... | collective-permute-start | bytes 442376 | tf_op jit(solution)/shard_map/ppermute | solution.py:8
  7.1 7.3 %collective-permute-start.1 = (bf16[64,1152]{1,0:T(8,128)(2,1)S(1)}, bf16[64,1152]{1,0:T(8,128)(2,1)S(1)}, u32[]{:S(2)}, u32[]{:S(2)}) collective-permute-start(bf16[64,1152]{1,0:T(8,128)(2,1)S(1)} %get-tuple-element.9), channel_id=1, source_target_pairs={{0,6},{2,4},{4,2},{6,0},{1,7},{3,5},{5,3},{7,1},{8,14},{10,12},{12... | collective-permute-start | bytes 442376 | tf_op jit(solution)/shard_map/ppermute | solution.py:8
  7.2 17.9 %collective-permute-start.13 = (bf16[128,1152]{1,0:T(8,128)(2,1)S(1)}, bf16[128,1152]{1,0:T(8,128)(2,1)S(1)}, u32[]{:S(2)}, u32[]{:S(2)}) collective-permute-start(bf16[128,1152]{1,0:T(8,128)(2,1)S(1)} %pad_maximum_fusion), channel_id=1, source_target_pairs={{0,1},{1,0},{2,3},{3,2},{4,5},{5,4},{6,7},{7,6},{8,9},{9,8},{10,11... | collective-permute-start | bytes 884744 | tf_op jit(solution)/shard_map/ppermute | solution.py:8
  14.5 13.1 %collective-permute-start.11 = (bf16[128,1152]{1,0:T(8,128)(2,1)S(1)}, bf16[128,1152]{1,0:T(8,128)(2,1)S(1)}, u32[]{:S(2)}, u32[]{:S(2)}) collective-permute-start(bf16[128,1152]{1,0:T(8,128)(2,1)S(1)} %constant_dynamic-update-slice_fusion), channel_id=1, source_target_pairs={{0,1},{1,0},{2,3},{3,2},{4,5},{5,4},{6,7},{7,6},{8,9},{9,8},{10,11... | collective-permute-start | bytes 884744 | tf_op jit(solution)/shard_map/ppermute | solution.py:8
  20.2 12.8 %collective-permute-start.7 = (bf16[64,3072]{1,0:T(8,128)(2,1)S(1)}, bf16[64,3072]{1,0:T(8,128)(2,1)S(1)}, u32[]{:S(2)}, u32[]{:S(2)}) collective-permute-start(bf16[64,3072]{1,0:T(8,128)(2,1)S(1)} %slice.97), channel_id=1, source_target_pairs={{0,2},{2,0},{4,6},{6,4},{1,3},{3,1},{5,7},{7,5},{8,10},{10,8},{12,... | collective-permute-start | bytes 1179656 | tf_op jit(solution)/shard_map/ppermute | solution.py:8
  21.9 8.3 %collective-permute-start.8 = (bf16[64,3072]{1,0:T(8,128)(2,1)S(1)}, bf16[64,3072]{1,0:T(8,128)(2,1)S(1)}, u32[]{:S(2)}, u32[]{:S(2)}) collective-permute-start(bf16[64,3072]{1,0:T(8,128)(2,1)S(1)} %slice.99), channel_id=1, source_target_pairs={{0,2},{2,0},{4,6},{6,4},{1,3},{3,1},{5,7},{7,5},{8,10},{10,8},{12,... | collective-permute-start | bytes 1179656 | tf_op jit(solution)/shard_map/ppermute | solution.py:8
  23.4 7.2 %collective-permute-start.4 = (bf16[64,3072]{1,0:T(8,128)(2,1)S(1)}, bf16[64,3072]{1,0:T(8,128)(2,1)S(1)}, u32[]{:S(2)}, u32[]{:S(2)}) collective-permute-start(bf16[64,3072]{1,0:T(8,128)(2,1)S(1)} %slice.95), channel_id=1, source_target_pairs={{0,2},{2,0},{4,6},{6,4},{1,3},{3,1},{5,7},{7,5},{8,10},{10,8},{12,... | collective-permute-start | bytes 1179656 | tf_op jit(solution)/shard_map/ppermute | solution.py:8
  25.0 21.2 %collective-permute-start.2 = (bf16[64,3072]{1,0:T(8,128)(2,1)S(1)}, bf16[64,3072]{1,0:T(8,128)(2,1)S(1)}, u32[]{:S(2)}, u32[]{:S(2)}) collective-permute-start(bf16[64,3072]{1,0:T(8,128)(2,1)S(1)} %slice.93), channel_id=1, source_target_pairs={{0,2},{2,0},{4,6},{6,4},{1,3},{3,1},{5,7},{7,5},{8,10},{10,8},{12,... | collective-permute-start | bytes 1179656 | tf_op jit(solution)/shard_map/ppermute | solution.py:8
  30.3 24.2 %collective-permute-start.12 = (bf16[64,6144]{1,0:T(8,128)(2,1)S(1)}, bf16[64,6144]{1,0:T(8,128)(2,1)S(1)}, u32[]{:S(2)}, u32[]{:S(2)}) collective-permute-start(bf16[64,6144]{1,0:T(8,128)(2,1)S(1)} %slice.101), channel_id=1, source_target_pairs={{0,2},{2,0},{4,6},{6,4},{1,3},{3,1},{5,7},{7,5},{8,10},{10,8},{12,... | collective-permute-start | bytes 2359304 | tf_op jit(solution)/shard_map/ppermute | solution.py:8
  30.6 12.1 %collective-permute-start.9 = (bf16[64,3072]{1,0:T(8,128)(2,1)S(1)}, bf16[64,3072]{1,0:T(8,128)(2,1)S(1)}, u32[]{:S(2)}, u32[]{:S(2)}) collective-permute-start(bf16[64,3072]{1,0:T(8,128)(2,1)S(1)} %add_convert_fusion.2), channel_id=1, source_target_pairs={{0,4},{2,6},{4,0},{6,2},{1,5},{3,7},{5,1},{7,3},{8,12},{10,14},{12... | collective-permute-start | bytes 1179656 | tf_op jit(solution)/shard_map/ppermute | solution.py:8
  32.3 18.8 %collective-permute-start.5 = (bf16[64,3072]{1,0:T(8,128)(2,1)S(1)}, bf16[64,3072]{1,0:T(8,128)(2,1)S(1)}, u32[]{:S(2)}, u32[]{:S(2)}) collective-permute-start(bf16[64,3072]{1,0:T(8,128)(2,1)S(1)} %add_convert_fusion.4), channel_id=1, source_target_pairs={{0,4},{2,6},{4,0},{6,2},{1,5},{3,7},{5,1},{7,3},{8,12},{10,14},{12... | collective-permute-start | bytes 1179656 | tf_op jit(solution)/shard_map/ppermute | solution.py:8
  33.0 34.9 %collective-permute-start.15 = (bf16[64,6144]{1,0:T(8,128)(2,1)S(1)}, bf16[64,6144]{1,0:T(8,128)(2,1)S(1)}, u32[]{:S(2)}, u32[]{:S(2)}) collective-permute-start(bf16[64,6144]{1,0:T(8,128)(2,1)S(1)} %add_convert_fusion), channel_id=1, source_target_pairs={{0,4},{2,6},{4,0},{6,2},{1,5},{3,7},{5,1},{7,3},{8,12},{10,14},{12... | collective-permute-start | bytes 2359304 | tf_op jit(solution)/shard_map/ppermute | solution.py:8
  44.6 31.7 %collective-permute-start.21 = (bf16[64,3072]{1,0:T(8,128)(2,1)S(1)}, bf16[64,3072]{1,0:T(8,128)(2,1)S(1)}, u32[]{:S(2)}, u32[]{:S(2)}) collective-permute-start(bf16[64,3072]{1,0:T(8,128)(2,1)S(1)} %fusion.79), channel_id=1, source_target_pairs={{0,4},{2,6},{4,0},{6,2},{1,5},{3,7},{5,1},{7,3},{8,12},{10,14},{12... | collective-permute-start | bytes 1179656 | tf_op jit(solution)/shard_map/ppermute | solution.py:8
  46.2 38.0 %collective-permute-start.10 = (bf16[64,3072]{1,0:T(8,128)(2,1)S(1)}, bf16[64,3072]{1,0:T(8,128)(2,1)S(1)}, u32[]{:S(2)}, u32[]{:S(2)}) collective-permute-start(bf16[64,3072]{1,0:T(8,128)(2,1)S(1)} %fusion.79), channel_id=1, source_target_pairs={{0,2},{2,0},{4,6},{6,4},{1,3},{3,1},{5,7},{7,5},{8,10},{10,8},{12,... | collective-permute-start | bytes 1179656 | tf_op jit(solution)/shard_map/ppermute | solution.py:8
  52.9 31.3 %collective-permute-start.19 = (bf16[64,3072]{1,0:T(8,128)(2,1)S(1)}, bf16[64,3072]{1,0:T(8,128)(2,1)S(1)}, u32[]{:S(2)}, u32[]{:S(2)}) collective-permute-start(bf16[64,3072]{1,0:T(8,128)(2,1)S(1)} %fusion.76), channel_id=1, source_target_pairs={{0,4},{2,6},{4,0},{6,2},{1,5},{3,7},{5,1},{7,3},{8,12},{10,14},{12... | collective-permute-start | bytes 1179656 | tf_op jit(solution)/shard_map/ppermute | solution.py:8
  71.6 18.6 %collective-permute-start.16 = (bf16[64,6144]{1,0:T(8,128)(2,1)S(1)}, bf16[64,6144]{1,0:T(8,128)(2,1)S(1)}, u32[]{:S(2)}, u32[]{:S(2)}) collective-permute-start(bf16[64,6144]{1,0:T(8,128)(2,1)S(1)} %fusion.54), channel_id=1, source_target_pairs={{0,2},{2,0},{4,6},{6,4},{1,3},{3,1},{5,7},{7,5},{8,10},{10,8},{12,... | collective-permute-start | bytes 2359304 | tf_op jit(solution)/shard_map/ppermute | solution.py:8
  71.7 38.2 %collective-permute-start.6 = (bf16[64,3072]{1,0:T(8,128)(2,1)S(1)}, bf16[64,3072]{1,0:T(8,128)(2,1)S(1)}, u32[]{:S(2)}, u32[]{:S(2)}) collective-permute-start(bf16[64,3072]{1,0:T(8,128)(2,1)S(1)} %fusion.76), channel_id=1, source_target_pairs={{0,2},{2,0},{4,6},{6,4},{1,3},{3,1},{5,7},{7,5},{8,10},{10,8},{12,... | collective-permute-start | bytes 1179656 | tf_op jit(solution)/shard_map/ppermute | solution.py:8
  76.3 32.3 %collective-permute-start.22 = (bf16[64,3072]{1,0:T(8,128)(2,1)S(1)}, bf16[64,3072]{1,0:T(8,128)(2,1)S(1)}, u32[]{:S(2)}, u32[]{:S(2)}) collective-permute-start(bf16[64,3072]{1,0:T(8,128)(2,1)S(1)} %collective-permute-done.21), channel_id=1, source_target_pairs={{0,2},{2,0},{4,6},{6,4},{1,3},{3,1},{5,7},{7,5},{8,10},{10,8},{12,... | collective-permute-start | bytes 1179656 | tf_op jit(solution)/shard_map/ppermute | solution.py:8
  84.2 31.6 %collective-permute-start.20 = (bf16[64,3072]{1,0:T(8,128)(2,1)S(1)}, bf16[64,3072]{1,0:T(8,128)(2,1)S(1)}, u32[]{:S(2)}, u32[]{:S(2)}) collective-permute-start(bf16[64,3072]{1,0:T(8,128)(2,1)S(1)} %collective-permute-done.19), channel_id=1, source_target_pairs={{0,2},{2,0},{4,6},{6,4},{1,3},{3,1},{5,7},{7,5},{8,10},{10,8},{12,... | collective-permute-start | bytes 1179656 | tf_op jit(solution)/shard_map/ppermute | solution.py:8
  88.6 20.0 %collective-permute-start.23 = (bf16[64,6144]{1,0:T(8,128)(2,1)S(1)}, bf16[64,6144]{1,0:T(8,128)(2,1)S(1)}, u32[]{:S(2)}, u32[]{:S(2)}) collective-permute-start(bf16[64,6144]{1,0:T(8,128)(2,1)S(1)} %fusion.54), channel_id=1, source_target_pairs={{0,4},{2,6},{4,0},{6,2},{1,5},{3,7},{5,1},{7,3},{8,12},{10,14},{12... | collective-permute-start | bytes 2359304 | tf_op jit(solution)/shard_map/ppermute | solution.py:8
  97.5 12.3 %collective-permute-start.17 = (bf16[128,1152]{1,0:T(8,128)(2,1)S(1)}, bf16[128,1152]{1,0:T(8,128)(2,1)S(1)}, u32[]{:S(2)}, u32[]{:S(2)}) collective-permute-start(bf16[128,1152]{1,0:T(8,128)(2,1)S(1)} %convolution_convert_fusion.3), channel_id=1, source_target_pairs={{0,1},{1,0},{2,3},{3,2},{4,5},{5,4},{6,7},{7,6},{8,9},{9,8},{10,11... | collective-permute-start | bytes 884744 | tf_op jit(solution)/shard_map/ppermute | solution.py:8
  113.4 9.5 %collective-permute-start.25 = (bf16[128,1152]{1,0:T(8,128)(2,1)S(1)}, bf16[128,1152]{1,0:T(8,128)(2,1)S(1)}, u32[]{:S(2)}, u32[]{:S(2)}) collective-permute-start(bf16[128,1152]{1,0:T(8,128)(2,1)S(1)} %convolution_convert_fusion.2), channel_id=1, source_target_pairs={{0,1},{1,0},{2,3},{3,2},{4,5},{5,4},{6,7},{7,6},{8,9},{9,8},{10,11... | collective-permute-start | bytes 884744 | tf_op jit(solution)/shard_map/ppermute | solution.py:8
  113.9 10.5 %collective-permute-start.18 = (bf16[64,1152]{1,0:T(8,128)(2,1)S(1)}, bf16[64,1152]{1,0:T(8,128)(2,1)S(1)}, u32[]{:S(2)}, u32[]{:S(2)}) collective-permute-start(bf16[64,1152]{1,0:T(8,128)(2,1)S(1)} %get-tuple-element.14), channel_id=1, source_target_pairs={{0,6},{2,4},{4,2},{6,0},{1,7},{3,5},{5,3},{7,1},{8,14},{10,12},{12... | collective-permute-start | bytes 442376 | tf_op jit(solution)/shard_map/ppermute | solution.py:8
  115.5 8.8 %collective-permute-start.27 = (bf16[64,1152]{1,0:T(8,128)(2,1)S(1)}, bf16[64,1152]{1,0:T(8,128)(2,1)S(1)}, u32[]{:S(2)}, u32[]{:S(2)}) collective-permute-start(bf16[64,1152]{1,0:T(8,128)(2,1)S(1)} %get-tuple-element.13), channel_id=1, source_target_pairs={{0,4},{2,6},{4,0},{6,2},{1,5},{3,7},{5,1},{7,3},{8,12},{10,14},{12... | collective-permute-start | bytes 442376 | tf_op jit(solution)/shard_map/ppermute | solution.py:8
  (12 other events, 139.8 us)
where the time goes:
time: 127 us
  waiting for transfers between devices  62.8 us (49%)
  matrix products  30 us (24%)
  starting transfers between devices  20.3 us (16%)
  other arithmetic  12.8 us (10%)
    ppermute x28, waiting for transfers between devices, swap(): return lax.ppermute(value, axis, [(i, i ^ mask) for i in range(size)])  62.8 us
    ppermute x28, starting transfers between devices, swap(): return lax.ppermute(value, axis, [(i, i ^ mask) for i in range(size)])  20.3 us
    dot_general x6, matrix products, down(): return jnp.dot(hidden, w_out[cut], preferred_element_type=jnp.float32)  17.7 us
    dot_general x6, matrix products, up(): jnp.dot(panel, w_in[:, cut], preferred_element_type=jnp.float32)  12.2 us
    convert_element_type x3, other arithmetic, local(): jax.nn.gelu(preact, approximate=False).astype(jnp.bfloat16)  7.5 us
  transfers between devices with their start and end apart: 28, of which 10 were waited for; matrix products, arithmetic and copies ran while one was open for 30% of the time, Pallas kernels for 0%

commit v1 on v0

--- a/solution.py
+++ b/solution.py
@@ -6,6 +6,10 @@
 
 def swap(value, axis, size, mask):
     return lax.ppermute(value, axis, [(i, i ^ mask) for i in range(size)])
+
+
+def after(value, other):
+    return value if other is None else lax.optimization_barrier((value, other))[0]
 
 
 def pick(blocks, index, slot):
@@ -73,15 +77,22 @@
         for q in range(cols):
             cuts = halves if q == 0 else whole
             hidden[q] = []
+            sent = None
             for cut in cuts:
-                away = swap(low_reduce(up(near_in[q], cut)), "row", rows, top)
+                sent = low_reduce(up(after(near_in[q], sent), cut))
+                away = swap(sent, "row", rows, top)
                 kept = low_reduce(up(far_in[q], cut))
                 preact = kept.astype(jnp.float32) + away.astype(jnp.float32) + b_in[cut]
                 hidden[q].append(jax.nn.gelu(preact, approximate=False).astype(jnp.bfloat16))
             far_out[q] = sum(down(low_gather(h), cut) for h, cut in zip(hidden[q], cuts))
         for q in reversed(range(cols)):
             cuts = halves if q == 0 else whole
-            near_out[q] = sum(down(low_gather(swap(h, "row", rows, top)), cut) for h, cut in zip(hidden[q], cuts))
+            total = None
+            for h, cut in zip(hidden[q], cuts):
+                back = after(swap(h, "row", rows, top), total)
+                part = down(low_gather(back), cut)
+                total = part if total is None else total + part
+            near_out[q] = total
 
         def finish(parts):
             total = parts[0]

time: 127 us -> 124 us (0.976)
  waiting for transfers between devices: 62.8 us -> 61.1 us
    ppermute x28, waiting for transfers between devices: 62.8 us -> 61.1 us  [swap(): return lax.ppermute(value, axis, [(i, i ^ mask) for i in range(size)])]
  transfers between devices with their start and end apart: 28 -> 28, of which waited for: 10 -> 9; matrix products, arithmetic and copies ran while one was open for 30% -> 30% of each run, Pallas kernels for 0% -> 0%
where the time goes in v1:
time: 124 us
  waiting for transfers between devices  61.1 us (49%)
  matrix products  29.6 us (24%)
  starting transfers between devices  19.8 us (16%)
  other arithmetic  12.8 us (10%)
    ppermute x28, waiting for transfers between devices, swap(): return lax.ppermute(value, axis, [(i, i ^ mask) for i in range(size)])  61.1 us
    ppermute x28, starting transfers between devices, swap(): return lax.ppermute(value, axis, [(i, i ^ mask) for i in range(size)])  19.8 us
    dot_general x6, matrix products, down(): return jnp.dot(hidden, w_out[cut], preferred_element_type=jnp.float32)  17.4 us
    dot_general x6, matrix products, up(): jnp.dot(panel, w_in[:, cut], preferred_element_type=jnp.float32)  12.2 us
    convert_element_type x3, other arithmetic, local(): jax.nn.gelu(preact, approximate=False).astype(jnp.bfloat16)  7.5 us
  transfers between devices with their start and end apart: 28, of which 9 were waited for; matrix products, arithmetic and copies ran while one was open for 30% of the time, Pallas kernels for 0%

profile of v1, /device:TPU:0, one launch (start us, length us, event | category | flops | bytes accessed | tf_op | source)
XLA Modules:
  0.0 124.1 jit_solution(14778927514843862065)
XLA Ops:
  4.5 2.6 %collective-permute-start = (bf16[64,1152]{1,0:T(8,128)(2,1)S(1)}, bf16[64,1152]{1,0:T(8,128)(2,1)S(1)}, u32[]{:S(2)}, u32[]{:S(2)}) collective-permute-start(bf16[64,1152]{1,0:T(8,128)(2,1)S(1)} %get-tuple-element.16), channel_id=1, source_target_pairs={{0,4},{2,6},{4,0},{6,2},{1,5},{3,7},{5,1},{7,3},{8,12},{10,14},{12... | collective-permute-start | bytes 442376 | tf_op jit(solution)/shard_map/ppermute | solution.py:8
  7.2 1.8 %collective-permute-start.13 = (bf16[128,1152]{1,0:T(8,128)(2,1)S(1)}, bf16[128,1152]{1,0:T(8,128)(2,1)S(1)}, u32[]{:S(2)}, u32[]{:S(2)}) collective-permute-start(bf16[128,1152]{1,0:T(8,128)(2,1)S(1)} %pad_maximum_fusion), channel_id=1, source_target_pairs={{0,1},{1,0},{2,3},{3,2},{4,5},{5,4},{6,7},{7,6},{8,9},{9,8},{10,11... | collective-permute-start | bytes 884744 | tf_op jit(solution)/shard_map/ppermute | solution.py:8
  9.0 2.8 %collective-permute-done = bf16[64,1152]{1,0:T(8,128)(2,1)S(1)} collective-permute-done((bf16[64,1152]{1,0:T(8,128)(2,1)S(1)}, bf16[64,1152]{1,0:T(8,128)(2,1)S(1)}, u32[]{:S(2)}, u32[]{:S(2)}) %collective-permute-start) | collective-permute-done | bytes 147488 | tf_op jit(solution)/shard_map/ppermute | solution.py:8
  11.8 2.6 %collective-permute-done.1 = bf16[64,1152]{1,0:T(8,128)(2,1)S(1)} collective-permute-done((bf16[64,1152]{1,0:T(8,128)(2,1)S(1)}, bf16[64,1152]{1,0:T(8,128)(2,1)S(1)}, u32[]{:S(2)}, u32[]{:S(2)}) %collective-permute-start.1) | collective-permute-done | bytes 147488 | tf_op jit(solution)/shard_map/ppermute | solution.py:8
  14.5 1.5 %collective-permute-start.11 = (bf16[128,1152]{1,0:T(8,128)(2,1)S(1)}, bf16[128,1152]{1,0:T(8,128)(2,1)S(1)}, u32[]{:S(2)}, u32[]{:S(2)}) collective-permute-start(bf16[128,1152]{1,0:T(8,128)(2,1)S(1)} %constant_dynamic-update-slice_fusion), channel_id=1, source_target_pairs={{0,1},{1,0},{2,3},{3,2},{4,5},{5,4},{6,7},{7,6},{8,9},{9,8},{10,11... | collective-permute-start | bytes 884744 | tf_op jit(solution)/shard_map/ppermute | solution.py:8
  16.0 4.2 %fusion.16 = bf16[128,3072]{1,0:T(8,128)(2,1)S(1)} fusion(bf16[128,1152]{1,0:T(8,128)(2,1)S(1)} %constant_dynamic-update-slice_fusion, bf16[1152,6144]{1,0:T(8,128)(2,1)} %param.8), kind=kOutput, calls=%fused_computation.18 | convolution fusion | flops 906362880 | bytes 8159232 | tf_op jit(solution)/shard_map/dot_general | solution.py:70
  23.8 2.2 %convolution_convert_fusion = bf16[128,6144]{1,0:T(8,128)(2,1)S(1)} fusion(bf16[128,1152]{1,0:T(8,128)(2,1)S(1)} %collective-permute-done.13, bf16[1152,6144]{1,0:T(8,128)(2,1)S(1)} %copy-done), kind=kOutput, calls=%fused_computation | convolution fusion | flops 1812725760 | bytes 16023552 | tf_op jit(solution)/shard_map/dot_general | solution.py:70
  26.2 2.2 %convolution_convert_fusion.1 = bf16[128,6144]{1,0:T(8,128)(2,1)S(1)} fusion(bf16[128,1152]{1,0:T(8,128)(2,1)S(1)} %collective-permute-done.11, bf16[1152,6144]{1,0:T(8,128)(2,1)S(1)} %copy-done), kind=kOutput, calls=%fused_computation.1 | convolution fusion | flops 1812725760 | bytes 16023552 | tf_op jit(solution)/shard_map/dot_general | solution.py:70
  29.1 1.6 %collective-permute-start.5 = (bf16[64,3072]{1,0:T(8,128)(2,1)S(1)}, bf16[64,3072]{1,0:T(8,128)(2,1)S(1)}, u32[]{:S(2)}, u32[]{:S(2)}) collective-permute-start(bf16[64,3072]{1,0:T(8,128)(2,1)S(1)} %add_convert_fusion.4), channel_id=1, source_target_pairs={{0,4},{2,6},{4,0},{6,2},{1,5},{3,7},{5,1},{7,3},{8,12},{10,14},{12... | collective-permute-start | bytes 1179656 | tf_op jit(solution)/shard_map/ppermute | solution.py:8
  32.8 8.4 %collective-permute-done.5 = bf16[64,3072]{1,0:T(8,128)(2,1)S(1)} collective-permute-done((bf16[64,3072]{1,0:T(8,128)(2,1)S(1)}, bf16[64,3072]{1,0:T(8,128)(2,1)S(1)}, u32[]{:S(2)}, u32[]{:S(2)}) %collective-permute-start.5) | collective-permute-done | bytes 393248 | tf_op jit(solution)/shard_map/ppermute | solution.py:8
  41.1 2.0 %fusion.76 = bf16[64,3072]{1,0:T(8,128)(2,1)S(1)} fusion(bf16[64,3072]{1,0:T(8,128)(2,1)S(1)} %collective-permute-done.5, bf16[64,3072]{1,0:T(8,128)(2,1)S(1)} %collective-permute-done.2, bf16[128,3072]{1,0:T(8,128)(2,1)S(1)} %fusion.16, f32[3072]{0:T(1024)S(1)} %get-tuple-element.20), kind=kLoop, calls=%fused_computation.73 | loop fusion | flops 14352384 | bytes 1585152 | tf_op jit(solution)/shard_map/convert_element_type | solution.py:86
  43.1 1.6 %collective-permute-start.19 = (bf16[64,3072]{1,0:T(8,128)(2,1)S(1)}, bf16[64,3072]{1,0:T(8,128)(2,1)S(1)}, u32[]{:S(2)}, u32[]{:S(2)}) collective-permute-start(bf16[64,3072]{1,0:T(8,128)(2,1)S(1)} %fusion.76), channel_id=1, source_target_pairs={{0,4},{2,6},{4,0},{6,2},{1,5},{3,7},{5,1},{7,3},{8,12},{10,14},{12... | collective-permute-start | bytes 1179656 | tf_op jit(solution)/shard_map/ppermute | solution.py:8
  45.4 21.0 %collective-permute-done.19 = bf16[64,3072]{1,0:T(8,128)(2,1)S(1)} collective-permute-done((bf16[64,3072]{1,0:T(8,128)(2,1)S(1)}, bf16[64,3072]{1,0:T(8,128)(2,1)S(1)}, u32[]{:S(2)}, u32[]{:S(2)}) %collective-permute-start.19) | collective-permute-done | bytes 393248 | tf_op jit(solution)/shard_map/ppermute | solution.py:8
  66.4 3.7 %fusion.54 = bf16[64,6144]{1,0:T(8,128)(2,1)S(1)} fusion(bf16[64,6144]{1,0:T(8,128)(2,1)S(1)} %collective-permute-done.15, bf16[64,6144]{1,0:T(8,128)(2,1)S(1)} %collective-permute-done.12, bf16[128,6144]{1,0:T(8,128)(2,1)S(1)} %convolution_convert_fusion.1, f32[6144]{0:T(1024)S(1)} %copy-done.2), kind=kLoop, calls=%fused_computation.38 | loop fusion | flops 28704768 | bytes 3170304 | tf_op jit(solution)/shard_map/convert_element_type | solution.py:86
  70.7 3.3 %collective-permute-done.9 = bf16[64,3072]{1,0:T(8,128)(2,1)S(1)} collective-permute-done((bf16[64,3072]{1,0:T(8,128)(2,1)S(1)}, bf16[64,3072]{1,0:T(8,128)(2,1)S(1)}, u32[]{:S(2)}, u32[]{:S(2)}) %collective-permute-start.9) | collective-permute-done | bytes 393248 | tf_op jit(solution)/shard_map/ppermute | solution.py:8
  74.0 1.8 %fusion.79 = bf16[64,3072]{1,0:T(8,128)(2,1)S(1)} fusion(bf16[64,3072]{1,0:T(8,128)(2,1)S(1)} %collective-permute-done.9, bf16[64,3072]{1,0:T(8,128)(2,1)S(1)} %collective-permute-done.7, bf16[128,3072]{1,0:T(8,128)(2,1)S(1)} %fusion.22, f32[3072]{0:T(1024)S(1)} %get-tuple-element.19), kind=kLoop, calls=%fused_computation.76 | loop fusion | flops 14352384 | bytes 1585152 | tf_op jit(solution)/shard_map/convert_element_type | solution.py:86
  75.8 1.6 %collective-permute-start.21 = (bf16[64,3072]{1,0:T(8,128)(2,1)S(1)}, bf16[64,3072]{1,0:T(8,128)(2,1)S(1)}, u32[]{:S(2)}, u32[]{:S(2)}) collective-permute-start(bf16[64,3072]{1,0:T(8,128)(2,1)S(1)} %fusion.79), channel_id=1, source_target_pairs={{0,4},{2,6},{4,0},{6,2},{1,5},{3,7},{5,1},{7,3},{8,12},{10,14},{12... | collective-permute-start | bytes 1179656 | tf_op jit(solution)/shard_map/ppermute | solution.py:8
  77.4 4.4 %fusion.8 = f32[128,1152]{1,0:T(8,128)S(1)} fusion(bf16[6144,1152]{1,0:T(8,128)(2,1)} %param.10, bf16[64,3072]{1,0:T(8,128)(2,1)S(1)} %collective-permute-done.20, bf16[64,3072]{1,0:T(8,128)(2,1)S(1)} %collective-permute-done.19), kind=kOutput, calls=%fused_computation.10 | convolution fusion | flops 907542528 | bytes 8454144 | tf_op jit(solution)/shard_map/dot_general | solution.py:73
  81.8 4.4 %collective-permute-done.21 = bf16[64,3072]{1,0:T(8,128)(2,1)S(1)} collective-permute-done((bf16[64,3072]{1,0:T(8,128)(2,1)S(1)}, bf16[64,3072]{1,0:T(8,128)(2,1)S(1)}, u32[]{:S(2)}, u32[]{:S(2)}) %collective-permute-start.21) | collective-permute-done | bytes 393248 | tf_op jit(solution)/shard_map/ppermute | solution.py:8
  86.2 1.5 %collective-permute-start.23 = (bf16[64,6144]{1,0:T(8,128)(2,1)S(1)}, bf16[64,6144]{1,0:T(8,128)(2,1)S(1)}, u32[]{:S(2)}, u32[]{:S(2)}) collective-permute-start(bf16[64,6144]{1,0:T(8,128)(2,1)S(1)} %fusion.54), channel_id=1, source_target_pairs={{0,4},{2,6},{4,0},{6,2},{1,5},{3,7},{5,1},{7,3},{8,12},{10,14},{12... | collective-permute-start | bytes 2359304 | tf_op jit(solution)/shard_map/ppermute | solution.py:8
  87.7 7.2 %convolution_convert_fusion.3 = bf16[128,1152]{1,0:T(8,128)(2,1)S(1)} fusion(bf16[6144,1152]{1,0:T(8,128)(2,1)} %param.10, bf16[64,6144]{1,0:T(8,128)(2,1)S(1)} %collective-permute-done.16, bf16[64,6144]{1,0:T(8,128)(2,1)S(1)} %fusion.54), kind=kOutput, calls=%fused_computation.31 | convolution fusion | flops 1815232512 | bytes 16023552 | tf_op jit(solution)/shard_map/dot_general | solution.py:73
  95.6 10.6 %collective-permute-done.23 = bf16[64,6144]{1,0:T(8,128)(2,1)S(1)} collective-permute-done((bf16[64,6144]{1,0:T(8,128)(2,1)S(1)}, bf16[64,6144]{1,0:T(8,128)(2,1)S(1)}, u32[]{:S(2)}, u32[]{:S(2)}) %collective-permute-start.23) | collective-permute-done | bytes 786464 | tf_op jit(solution)/shard_map/ppermute | solution.py:8
  108.7 2.2 %convolution_convert_fusion.2 = bf16[128,1152]{1,0:T(8,128)(2,1)S(1)} fusion(bf16[6144,1152]{1,0:T(8,128)(2,1)S(1)} %bitcast.10, bf16[64,6144]{1,0:T(8,128)(2,1)S(1)} %collective-permute-done.24, bf16[64,6144]{1,0:T(8,128)(2,1)S(1)} %collective-permute-done.23), kind=kOutput, calls=%fused_computation.30 | convolution fusion | flops 1815232512 | bytes 16023552 | tf_op jit(solution)/shard_map/dot_general | solution.py:73
  113.8 6.6 %collective-permute-done.25 = bf16[128,1152]{1,0:T(8,128)(2,1)S(1)} collective-permute-done((bf16[128,1152]{1,0:T(8,128)(2,1)S(1)}, bf16[128,1152]{1,0:T(8,128)(2,1)S(1)}, u32[]{:S(2)}, u32[]{:S(2)}) %collective-permute-start.25) | collective-permute-done | bytes 294944 | tf_op jit(solution)/shard_map/ppermute | solution.py:8
  (87 shorter events, 21.9 us)
Async XLA Ops:
  4.5 7.3 %collective-permute-start = (bf16[64,1152]{1,0:T(8,128)(2,1)S(1)}, bf16[64,1152]{1,0:T(8,128)(2,1)S(1)}, u32[]{:S(2)}, u32[]{:S(2)}) collective-permute-start(bf16[64,1152]{1,0:T(8,128)(2,1)S(1)} %get-tuple-element.16), channel_id=1, source_target_pairs={{0,4},{2,6},{4,0},{6,2},{1,5},{3,7},{5,1},{7,3},{8,12},{10,14},{12... | collective-permute-start | bytes 442376 | tf_op jit(solution)/shard_map/ppermute | solution.py:8
  7.1 7.3 %collective-permute-start.1 = (bf16[64,1152]{1,0:T(8,128)(2,1)S(1)}, bf16[64,1152]{1,0:T(8,128)(2,1)S(1)}, u32[]{:S(2)}, u32[]{:S(2)}) collective-permute-start(bf16[64,1152]{1,0:T(8,128)(2,1)S(1)} %get-tuple-element.13), channel_id=1, source_target_pairs={{0,6},{2,4},{4,2},{6,0},{1,7},{3,5},{5,3},{7,1},{8,14},{10,12},{12... | collective-permute-start | bytes 442376 | tf_op jit(solution)/shard_map/ppermute | solution.py:8
  7.2 16.6 %collective-permute-start.13 = (bf16[128,1152]{1,0:T(8,128)(2,1)S(1)}, bf16[128,1152]{1,0:T(8,128)(2,1)S(1)}, u32[]{:S(2)}, u32[]{:S(2)}) collective-permute-start(bf16[128,1152]{1,0:T(8,128)(2,1)S(1)} %pad_maximum_fusion), channel_id=1, source_target_pairs={{0,1},{1,0},{2,3},{3,2},{4,5},{5,4},{6,7},{7,6},{8,9},{9,8},{10,11... | collective-permute-start | bytes 884744 | tf_op jit(solution)/shard_map/ppermute | solution.py:8
  14.5 11.8 %collective-permute-start.11 = (bf16[128,1152]{1,0:T(8,128)(2,1)S(1)}, bf16[128,1152]{1,0:T(8,128)(2,1)S(1)}, u32[]{:S(2)}, u32[]{:S(2)}) collective-permute-start(bf16[128,1152]{1,0:T(8,128)(2,1)S(1)} %constant_dynamic-update-slice_fusion), channel_id=1, source_target_pairs={{0,1},{1,0},{2,3},{3,2},{4,5},{5,4},{6,7},{7,6},{8,9},{9,8},{10,11... | collective-permute-start | bytes 884744 | tf_op jit(solution)/shard_map/ppermute | solution.py:8
  20.2 12.0 %collective-permute-start.2 = (bf16[64,3072]{1,0:T(8,128)(2,1)S(1)}, bf16[64,3072]{1,0:T(8,128)(2,1)S(1)}, u32[]{:S(2)}, u32[]{:S(2)}) collective-permute-start(bf16[64,3072]{1,0:T(8,128)(2,1)S(1)} %slice.93), channel_id=1, source_target_pairs={{0,2},{2,0},{4,6},{6,4},{1,3},{3,1},{5,7},{7,5},{8,10},{10,8},{12,... | collective-permute-start | bytes 1179656 | tf_op jit(solution)/shard_map/ppermute | solution.py:8
  21.9 7.1 %collective-permute-start.4 = (bf16[64,3072]{1,0:T(8,128)(2,1)S(1)}, bf16[64,3072]{1,0:T(8,128)(2,1)S(1)}, u32[]{:S(2)}, u32[]{:S(2)}) collective-permute-start(bf16[64,3072]{1,0:T(8,128)(2,1)S(1)} %slice.95), channel_id=1, source_target_pairs={{0,2},{2,0},{4,6},{6,4},{1,3},{3,1},{5,7},{7,5},{8,10},{10,8},{12,... | collective-permute-start | bytes 1179656 | tf_op jit(solution)/shard_map/ppermute | solution.py:8
  23.3 47.4 %collective-permute-start.7 = (bf16[64,3072]{1,0:T(8,128)(2,1)S(1)}, bf16[64,3072]{1,0:T(8,128)(2,1)S(1)}, u32[]{:S(2)}, u32[]{:S(2)}) collective-permute-start(bf16[64,3072]{1,0:T(8,128)(2,1)S(1)} %slice.97), channel_id=1, source_target_pairs={{0,2},{2,0},{4,6},{6,4},{1,3},{3,1},{5,7},{7,5},{8,10},{10,8},{12,... | collective-permute-start | bytes 1179656 | tf_op jit(solution)/shard_map/ppermute | solution.py:8
  28.5 16.3 %collective-permute-start.12 = (bf16[64,6144]{1,0:T(8,128)(2,1)S(1)}, bf16[64,6144]{1,0:T(8,128)(2,1)S(1)}, u32[]{:S(2)}, u32[]{:S(2)}) collective-permute-start(bf16[64,6144]{1,0:T(8,128)(2,1)S(1)} %slice.101), channel_id=1, source_target_pairs={{0,2},{2,0},{4,6},{6,4},{1,3},{3,1},{5,7},{7,5},{8,10},{10,8},{12,... | collective-permute-start | bytes 2359304 | tf_op jit(solution)/shard_map/ppermute | solution.py:8
  29.1 12.1 %collective-permute-start.5 = (bf16[64,3072]{1,0:T(8,128)(2,1)S(1)}, bf16[64,3072]{1,0:T(8,128)(2,1)S(1)}, u32[]{:S(2)}, u32[]{:S(2)}) collective-permute-start(bf16[64,3072]{1,0:T(8,128)(2,1)S(1)} %add_convert_fusion.4), channel_id=1, source_target_pairs={{0,4},{2,6},{4,0},{6,2},{1,5},{3,7},{5,1},{7,3},{8,12},{10,14},{12... | collective-permute-start | bytes 1179656 | tf_op jit(solution)/shard_map/ppermute | solution.py:8
  31.9 12.8 %collective-permute-start.8 = (bf16[64,3072]{1,0:T(8,128)(2,1)S(1)}, bf16[64,3072]{1,0:T(8,128)(2,1)S(1)}, u32[]{:S(2)}, u32[]{:S(2)}) collective-permute-start(bf16[64,3072]{1,0:T(8,128)(2,1)S(1)} %slice.99), channel_id=1, source_target_pairs={{0,2},{2,0},{4,6},{6,4},{1,3},{3,1},{5,7},{7,5},{8,10},{10,8},{12,... | collective-permute-start | bytes 1179656 | tf_op jit(solution)/shard_map/ppermute | solution.py:8
  32.2 34.2 %collective-permute-start.15 = (bf16[64,6144]{1,0:T(8,128)(2,1)S(1)}, bf16[64,6144]{1,0:T(8,128)(2,1)S(1)}, u32[]{:S(2)}, u32[]{:S(2)}) collective-permute-start(bf16[64,6144]{1,0:T(8,128)(2,1)S(1)} %add_convert_fusion), channel_id=1, source_target_pairs={{0,4},{2,6},{4,0},{6,2},{1,5},{3,7},{5,1},{7,3},{8,12},{10,14},{12... | collective-permute-start | bytes 2359304 | tf_op jit(solution)/shard_map/ppermute | solution.py:8
  43.1 23.3 %collective-permute-start.19 = (bf16[64,3072]{1,0:T(8,128)(2,1)S(1)}, bf16[64,3072]{1,0:T(8,128)(2,1)S(1)}, u32[]{:S(2)}, u32[]{:S(2)}) collective-permute-start(bf16[64,3072]{1,0:T(8,128)(2,1)S(1)} %fusion.76), channel_id=1, source_target_pairs={{0,4},{2,6},{4,0},{6,2},{1,5},{3,7},{5,1},{7,3},{8,12},{10,14},{12... | collective-permute-start | bytes 1179656 | tf_op jit(solution)/shard_map/ppermute | solution.py:8
  44.7 62.7 %collective-permute-start.6 = (bf16[64,3072]{1,0:T(8,128)(2,1)S(1)}, bf16[64,3072]{1,0:T(8,128)(2,1)S(1)}, u32[]{:S(2)}, u32[]{:S(2)}) collective-permute-start(bf16[64,3072]{1,0:T(8,128)(2,1)S(1)} %fusion.76), channel_id=1, source_target_pairs={{0,2},{2,0},{4,6},{6,4},{1,3},{3,1},{5,7},{7,5},{8,10},{10,8},{12,... | collective-permute-start | bytes 1179656 | tf_op jit(solution)/shard_map/ppermute | solution.py:8
  44.8 29.2 %collective-permute-start.9 = (bf16[64,3072]{1,0:T(8,128)(2,1)S(1)}, bf16[64,3072]{1,0:T(8,128)(2,1)S(1)}, u32[]{:S(2)}, u32[]{:S(2)}) collective-permute-start(bf16[64,3072]{1,0:T(8,128)(2,1)S(1)} %add_convert_fusion.2), channel_id=1, source_target_pairs={{0,4},{2,6},{4,0},{6,2},{1,5},{3,7},{5,1},{7,3},{8,12},{10,14},{12... | collective-permute-start | bytes 1179656 | tf_op jit(solution)/shard_map/ppermute | solution.py:8
  66.4 11.0 %collective-permute-start.20 = (bf16[64,3072]{1,0:T(8,128)(2,1)S(1)}, bf16[64,3072]{1,0:T(8,128)(2,1)S(1)}, u32[]{:S(2)}, u32[]{:S(2)}) collective-permute-start(bf16[64,3072]{1,0:T(8,128)(2,1)S(1)} %collective-permute-done.19), channel_id=1, source_target_pairs={{0,2},{2,0},{4,6},{6,4},{1,3},{3,1},{5,7},{7,5},{8,10},{10,8},{12,... | collective-permute-start | bytes 1179656 | tf_op jit(solution)/shard_map/ppermute | solution.py:8
  70.1 17.6 %collective-permute-start.16 = (bf16[64,6144]{1,0:T(8,128)(2,1)S(1)}, bf16[64,6144]{1,0:T(8,128)(2,1)S(1)}, u32[]{:S(2)}, u32[]{:S(2)}) collective-permute-start(bf16[64,6144]{1,0:T(8,128)(2,1)S(1)} %fusion.54), channel_id=1, source_target_pairs={{0,2},{2,0},{4,6},{6,4},{1,3},{3,1},{5,7},{7,5},{8,10},{10,8},{12,... | collective-permute-start | bytes 2359304 | tf_op jit(solution)/shard_map/ppermute | solution.py:8
  75.8 10.4 %collective-permute-start.21 = (bf16[64,3072]{1,0:T(8,128)(2,1)S(1)}, bf16[64,3072]{1,0:T(8,128)(2,1)S(1)}, u32[]{:S(2)}, u32[]{:S(2)}) collective-permute-start(bf16[64,3072]{1,0:T(8,128)(2,1)S(1)} %fusion.79), channel_id=1, source_target_pairs={{0,4},{2,6},{4,0},{6,2},{1,5},{3,7},{5,1},{7,3},{8,12},{10,14},{12... | collective-permute-start | bytes 1179656 | tf_op jit(solution)/shard_map/ppermute | solution.py:8
  77.4 28.7 %collective-permute-start.10 = (bf16[64,3072]{1,0:T(8,128)(2,1)S(1)}, bf16[64,3072]{1,0:T(8,128)(2,1)S(1)}, u32[]{:S(2)}, u32[]{:S(2)}) collective-permute-start(bf16[64,3072]{1,0:T(8,128)(2,1)S(1)} %fusion.79), channel_id=1, source_target_pairs={{0,2},{2,0},{4,6},{6,4},{1,3},{3,1},{5,7},{7,5},{8,10},{10,8},{12,... | collective-permute-start | bytes 1179656 | tf_op jit(solution)/shard_map/ppermute | solution.py:8
  86.2 27.6 %collective-permute-start.22 = (bf16[64,3072]{1,0:T(8,128)(2,1)S(1)}, bf16[64,3072]{1,0:T(8,128)(2,1)S(1)}, u32[]{:S(2)}, u32[]{:S(2)}) collective-permute-start(bf16[64,3072]{1,0:T(8,128)(2,1)S(1)} %collective-permute-done.21), channel_id=1, source_target_pairs={{0,2},{2,0},{4,6},{6,4},{1,3},{3,1},{5,7},{7,5},{8,10},{10,8},{12,... | collective-permute-start | bytes 1179656 | tf_op jit(solution)/shard_map/ppermute | solution.py:8
  86.2 20.0 %collective-permute-start.23 = (bf16[64,6144]{1,0:T(8,128)(2,1)S(1)}, bf16[64,6144]{1,0:T(8,128)(2,1)S(1)}, u32[]{:S(2)}, u32[]{:S(2)}) collective-permute-start(bf16[64,6144]{1,0:T(8,128)(2,1)S(1)} %fusion.54), channel_id=1, source_target_pairs={{0,4},{2,6},{4,0},{6,2},{1,5},{3,7},{5,1},{7,3},{8,12},{10,14},{12... | collective-permute-start | bytes 2359304 | tf_op jit(solution)/shard_map/ppermute | solution.py:8
  95.0 12.4 %collective-permute-start.17 = (bf16[128,1152]{1,0:T(8,128)(2,1)S(1)}, bf16[128,1152]{1,0:T(8,128)(2,1)S(1)}, u32[]{:S(2)}, u32[]{:S(2)}) collective-permute-start(bf16[128,1152]{1,0:T(8,128)(2,1)S(1)} %convolution_convert_fusion.3), channel_id=1, source_target_pairs={{0,1},{1,0},{2,3},{3,2},{4,5},{5,4},{6,7},{7,6},{8,9},{9,8},{10,11... | collective-permute-start | bytes 884744 | tf_op jit(solution)/shard_map/ppermute | solution.py:8
  110.9 9.5 %collective-permute-start.25 = (bf16[128,1152]{1,0:T(8,128)(2,1)S(1)}, bf16[128,1152]{1,0:T(8,128)(2,1)S(1)}, u32[]{:S(2)}, u32[]{:S(2)}) collective-permute-start(bf16[128,1152]{1,0:T(8,128)(2,1)S(1)} %convolution_convert_fusion.2), channel_id=1, source_target_pairs={{0,1},{1,0},{2,3},{3,2},{4,5},{5,4},{6,7},{7,6},{8,9},{9,8},{10,11... | collective-permute-start | bytes 884744 | tf_op jit(solution)/shard_map/ppermute | solution.py:8
  111.8 9.9 %collective-permute-start.18 = (bf16[64,1152]{1,0:T(8,128)(2,1)S(1)}, bf16[64,1152]{1,0:T(8,128)(2,1)S(1)}, u32[]{:S(2)}, u32[]{:S(2)}) collective-permute-start(bf16[64,1152]{1,0:T(8,128)(2,1)S(1)} %get-tuple-element.18), channel_id=1, source_target_pairs={{0,6},{2,4},{4,2},{6,0},{1,7},{3,5},{5,3},{7,1},{8,14},{10,12},{12... | collective-permute-start | bytes 442376 | tf_op jit(solution)/shard_map/ppermute | solution.py:8
  112.9 8.8 %collective-permute-start.27 = (bf16[64,1152]{1,0:T(8,128)(2,1)S(1)}, bf16[64,1152]{1,0:T(8,128)(2,1)S(1)}, u32[]{:S(2)}, u32[]{:S(2)}) collective-permute-start(bf16[64,1152]{1,0:T(8,128)(2,1)S(1)} %get-tuple-element.17), channel_id=1, source_target_pairs={{0,4},{2,6},{4,0},{6,2},{1,5},{3,7},{5,1},{7,3},{8,12},{10,14},{12... | collective-permute-start | bytes 442376 | tf_op jit(solution)/shard_map/ppermute | solution.py:8
  (12 other events, 158.2 us)
